TPU v7x, 32 devices: a whole 2x2x4 slice. The times are simulated.
32 devices in a mesh: inp: 8 (over z, y), tm: 4 (over x, core).
Axes of the slice: x: 2, y: 2, z: 4, core: 2. Of those that a mesh axis runs over, the one named last changes fastest.
Arguments:
- voltages: bfloat16 [1024, 262144], P('inp', 'tm'), may hold values from -6 to 6
- pfb_coeff: float32 [16, 512], replicated, may hold values from -1.5 to 1.5
Outputs:
- visibilities: float32 [32, 2, 1024, 1024], P(('inp', 'tm'))
All inputs are finite; a program needn't handle non-finite values.
Results may differ from a plain program's by a relative error of at most 0.0029.
Values may be sent and summed in bfloat16 or wider, within the bound.
No kernel may reach another device: no remote copies, remote signals or barrier semaphores. Data moves between devices by JAX's collectives and lax.ppermute only.
A program may use at most 128 MiB of HBM per device.

v0:
```python
import math

import jax
import jax.numpy as jnp
from jax import lax
from jax.sharding import PartitionSpec as P

CH_DEV = 1


def shifted(block, axis, distance):
    devices = range(lax.axis_size(axis))
    route = [(i - distance, i) for i in devices if i - distance in devices]
    return lax.ppermute(block, axis, route)


def dft_rows(channel_ids, length):
    samples = jnp.arange(length, dtype=jnp.int32)
    phase_index = channel_ids[:, None] * samples[None, :] % length
    phase_angle = phase_index.astype(jnp.float32) * (2.0 * math.pi / length)
    norm_scale = 1.0 / math.sqrt(length)
    cos_part = jnp.cos(phase_angle) * norm_scale
    sin_part = -jnp.sin(phase_angle) * norm_scale
    return jnp.stack([cos_part, sin_part], axis=1).reshape(2 * channel_ids.shape[0], length)


def correlate(received):
    item_count = received.shape[1]
    inputs_all = received.shape[3]
    spectra_all = received.shape[4]
    stacked = received.reshape(item_count, 2 * inputs_all, spectra_all)
    products = jnp.einsum("kas,kbs->kab", stacked, stacked, preferred_element_type=jnp.float32)
    real_sum = products[:, :inputs_all, :inputs_all] + products[:, inputs_all:, inputs_all:]
    imag_diff = products[:, inputs_all:, :inputs_all] - products[:, :inputs_all, inputs_all:]
    return jnp.stack([real_sum, imag_diff], axis=1) * (1.0 / spectra_all)


def per_device(voltages, pfb_coeff):
    in_rows = voltages.shape[0]
    tap_count = pfb_coeff.shape[0]
    length = pfb_coeff.shape[1]
    spec_dev = voltages.shape[1] // length
    groups_inp = lax.axis_size("inp")
    groups_tm = lax.axis_size("tm")
    channels = CH_DEV * groups_inp * groups_tm
    blocks = voltages.reshape(in_rows, spec_dev, length)
    tail_blocks = blocks[:, spec_dev - (tap_count - 1) :, :]
    history = shifted(tail_blocks, "tm", 1)
    extended = jnp.concatenate([history, blocks], axis=1)
    filtered = jnp.zeros((in_rows, spec_dev, length), jnp.float32)
    for tap_index in range(tap_count):
        filtered = filtered + pfb_coeff[tap_index][None, None, :] * extended[
            :, tap_index : tap_index + spec_dev, :
        ].astype(jnp.float32)
    positions = jnp.arange(channels, dtype=jnp.int32)
    dft_table = dft_rows(positions, length)
    spectra = jnp.einsum(
        "cn,asn->cas",
        dft_table,
        filtered,
        precision=lax.Precision.HIGHEST,
        preferred_element_type=jnp.float32,
    ).astype(jnp.bfloat16)
    outgoing = spectra.reshape(groups_inp, 2 * channels // groups_inp, in_rows, spec_dev)
    turned = lax.all_to_all(outgoing, "inp", split_axis=0, concat_axis=2, tiled=True)
    per_slab = turned.reshape(groups_tm, CH_DEV, 2, in_rows * groups_inp, spec_dev)
    result = correlate(lax.all_to_all(per_slab, "tm", split_axis=0, concat_axis=4, tiled=True))
    return result


def solution(mesh):
    return jax.shard_map(
        per_device,
        mesh=mesh,
        in_specs=(P("inp", "tm"), P()),
        out_specs=P(("inp", "tm"), None, None, None),
        check_vma=False,
    )
```

profile of v0, /device:TPU:0, one launch (start us, length us, event | category | flops | bytes accessed | tf_op | source)
XLA Modules:
  0.0 309.1 jit_solution(6881728016254690156)
XLA Ops:
  0.0 0.0 copy-start
  0.0 22.4 %copy.27 = bf16[128,65536]{0,1:T(8,128)(2,1)} copy(bf16[128,65536]{1,0:T(8,128)(2,1)} %param.2) | data formatting | bytes 33554432 | tf_op args[0]
  22.4 1.7 slice.144
  24.1 2.3 copy.28
  26.4 3.7 %collective-permute-start = (bf16[128,15,512]{2,0,1:T(8,128)(2,1)}, bf16[128,15,512]{2,0,1:T(8,128)(2,1)}, u32[]{:S(2)}, u32[]{:S(2)}) collective-permute-start(bf16[128,15,512]{2,0,1:T(8,128)(2,1)} %copy.28), channel_id=1, source_target_pairs={{0,1},{1,2},{2,3},{4,5},{5,6},{6,7},{8,9},{9,10},{10,11},{12,13},{... | collective-permute-start | bytes 5898248 | tf_op jit(solution)/shard_map/ppermute | solution.py:14
  30.0 0.3 negate_multiply_fusion
  30.3 0.1 copy.26
  30.4 0.1 reshape.154
  30.5 0.0 copy-done
  30.6 2.1 collective-permute-done
  32.7 2.8 copy.29
  35.5 91.2 %multiply_add_fusion = f32[128,128,512]{0,2,1:T(8,128)} fusion(bf16[128,128,512]{0,2,1:T(8,128)(2,1)} %bitcast.43, bf16[128,15,512]{0,2,1:T(8,128)(2,1)S(1)} %copy.29, f32[512]{0:T(512)S(1)} %bitcast.61, f32[512]{0:T(512)S(1)} %bitcast.62, f32[512]{0:T(512)S(1)} %bitcast.48, f32[512]{0:T(512)S(1)} %bitcast.49, f32[512]{0:T(512)S(1)} %bitcast.50, ...), kind=kLoop, calls=%fused_computation.14 | loop fusion | flops 520093696 | bytes 52330496 | tf_op jit(solution)/shard_map/add | solution.py:52
  126.7 34.6 %copy.30 = f32[128,128,512]{2,1,0:T(8,128)} copy(f32[128,128,512]{0,2,1:T(8,128)} %multiply_add_fusion) | data formatting | bytes 67108864 | tf_op jit(solution)/shard_map/add | solution.py:52
  161.3 35.3 %convert_bitcast_fusion = bf16[8,8,128,128]{3,1,0,2:T(8,128)(2,1)S(1)} fusion(f32[64,512,1]{1,0,2:T(8,128)S(1)} %reshape.154, f32[128,128,512]{2,1,0:T(8,128)} %copy.30), kind=kOutput, calls=%fused_computation.46 | convolution fusion | flops 6443499520 | bytes 35782656 | tf_op jit(solution)/shard_map/cn,asn->cas/dot_general | solution.py:57
  196.6 1.4 copy.31
  198.0 49.0 %all_to_all.30 = bf16[8,8,128,128]{3,2,1,0:T(8,128)(2,1)S(1)} all-to-all(bf16[8,8,128,128]{3,2,1,0:T(8,128)(2,1)S(1)} %copy.31), channel_id=1, replica_groups=mesh['inp'=8,'tm'=4] {'inp'}, dimensions={0} | all-to-all | bytes 4194304 | tf_op jit(solution)/shard_map/all_to_all | solution.py:65
  246.9 0.2 copy.32
  247.2 34.8 %all_to_all.31 = bf16[4,1,2,1024,128]{4,3,2,1,0:T(8,128)(2,1)S(1)} all-to-all(bf16[4,1,2,1024,128]{4,3,2,1,0:T(8,128)(2,1)S(1)} %bitcast.44), channel_id=1, replica_groups=mesh['inp'=8,'tm'=4] {'tm'}, dimensions={0} | all-to-all | bytes 4194304 | tf_op jit(solution)/shard_map/all_to_all | solution.py:67
  281.9 1.6 copy.34
  283.5 8.3 %convolution_bitcast_fusion = f32[1,2048,2048]{2,1,0:T(8,128)} fusion(bf16[256,8,4,128]{3,2,1,0:T(4,128)(2,1)S(1)} %bitcast.46), kind=kOutput, calls=%fused_computation.38 | convolution fusion | flops 4294967296 | bytes 18874368 | tf_op jit(solution)/shard_map/kas,kbs->kab/dot_general | solution.py:32
  291.8 10.3 %fusion.15 = (f32[1,1,1024,1024]{3,2,1,0:T(8,128)S(1)}, f32[1,1,1024,1024]{3,2,1,0:T(8,128)}) fusion(f32[1,2048,2048]{2,1,0:T(8,128)} %convolution_bitcast_fusion), kind=kLoop, calls=%fused_computation.43 | loop fusion | flops 2097152 | bytes 25165824 | tf_op jit(solution)/shard_map/stack | solution.py:35
  302.1 7.0 %maximum_multiply_fusion = f32[1,2,1024,1024]{3,2,1,0:T(8,128)} fusion(f32[1,1,1024,1024]{3,2,1,0:T(8,128)} %get-tuple-element.6, f32[1,1,1024,1024]{3,2,1,0:T(8,128)S(1)} %get-tuple-element.5), kind=kLoop, calls=%fused_computation.39 | loop fusion | flops 4194304 | bytes 16777216 | tf_op jit(solution)/shard_map/mul | solution.py:35
  (2 shorter events, 0.0 us)
Async XLA Ops:
  0.0 30.5 %copy-start = (f32[16,512]{1,0:T(8,128)S(1)}, f32[16,512]{1,0:T(8,128)}, u32[]{:S(2)}) copy-start(f32[16,512]{1,0:T(8,128)} %param.3) | copy-start | bytes 98308
  26.4 6.3 %collective-permute-start = (bf16[128,15,512]{2,0,1:T(8,128)(2,1)}, bf16[128,15,512]{2,0,1:T(8,128)(2,1)}, u32[]{:S(2)}, u32[]{:S(2)}) collective-permute-start(bf16[128,15,512]{2,0,1:T(8,128)(2,1)} %copy.28), channel_id=1, source_target_pairs={{0,1},{1,2},{2,3},{4,5},{5,6},{6,7},{8,9},{9,10},{10,11},{12,13},{... | collective-permute-start | bytes 5898248 | tf_op jit(solution)/shard_map/ppermute | solution.py:14
where the time goes:
time: 310 us; the launch traced here: 309 us
  other arithmetic  109 us (35%)
  blocking collectives  83.7 us (27%)
  local copies, waits for them, and re-layouts  67.2 us (22%)
  matrix products  43.5 us (14%)
  starting transfers between devices  3.69 us (1%)
    add x1, other arithmetic, per_device(): filtered + pfb_coeff[tap_index][None, None, :] * extended[:, tap_index:ta...  91.2 us
    all_to_all x1, blocking collectives, per_device(): lax.all_to_all(outgoing, 'inp', split_axis=0, concat_axis=2, tiled=True)  49 us
    dot_general x1, matrix products, per_device(): jnp.einsum('cn,asn->cas', dft_table, filtered, precision=lax.Precision.HI...  35.3 us
    all_to_all x1, blocking collectives, per_device(): lax.all_to_all(per_slab, 'tm', split_axis=0, concat_axis=4, tiled=True)  34.8 us
    add x1, local copies, waits for them, and re-layouts, per_device(): filtered + pfb_coeff[tap_index][None, None, :] * extended[:, tap_index:ta...  34.6 us
    unnamed x3, local copies, waits for them, and re-layouts  22.4 us
    another operation x1, other arithmetic, correlate(): return jnp.stack([real_sum, imag_diff], axis=1) * (1.0 / spectra_all)  10.3 us
    dot_general x1, matrix products, correlate(): jnp.einsum('kas,kbs->kab', stacked, stacked, preferred_element_type=jnp.f...  8.28 us
  transfers between devices with their start and end apart: 1, of which 1 were waited for; matrix products, arithmetic and copies ran while one was open for 0% of the time, Pallas kernels for 0%

commit v1 on v0

v1 whole, which is shorter than its diff:
```python
import functools
import math

import jax
import jax.numpy as jnp
import numpy as np
from jax import lax
from jax.experimental import pallas as pl
from jax.experimental.pallas import tpu as pltpu
from jax.sharding import PartitionSpec as P

CH_DEV = 1
STEP = 16
ROWS = 16
LANES = 128
VMEM_LIMIT = 60 * 1024 * 1024


def shifted(block, axis, distance):
    devices = range(lax.axis_size(axis))
    route = [(i - distance, i) for i in devices if i - distance in devices]
    return lax.ppermute(block, axis, route)


def dft_table(channels, length):
    samples = np.arange(length)
    angle = (np.arange(channels)[:, None] * samples[None, :] % length) * (2.0 * math.pi / length)
    table = np.stack([np.cos(angle), -np.sin(angle)], axis=1).reshape(2 * channels, length)
    table = (table / math.sqrt(length)).T
    high = table.astype(jnp.bfloat16)
    low = (table - high.astype(np.float64)).astype(jnp.bfloat16)
    both = np.concatenate([high, low], axis=1)
    return jnp.asarray(np.concatenate([both, both], axis=0))


def spectra_kernel(prev_ref, main_ref, coeff_ref, table_ref, out_ref, parts_ref, turn_ref, *, taps, length, offset):
    in_rows = main_ref.shape[0]
    width = out_ref.shape[0]
    tiles = length // LANES

    def block_at(position, row, lane):
        ref, first = (main_ref, position) if position >= 0 else (prev_ref, position + offset)
        return ref[pl.ds(row, ROWS), pl.ds(first * length + lane, LANES)].astype(jnp.float32)

    def filter_tile(index, carry):
        row = pl.multiple_of(index // tiles * ROWS, ROWS)
        lane = pl.multiple_of(index % tiles * LANES, LANES)
        gains = [coeff_ref[pl.ds(8 * j, 8), pl.ds(lane, LANES)] for j in range(taps)]
        sums = {}
        for position in range(1 - taps, STEP):
            block = block_at(position, row, lane)
            halves = [block[8 * k : 8 * k + 8] for k in range(ROWS // 8)]
            for j in range(taps):
                spectrum = position + taps - 1 - j
                if 0 <= spectrum < STEP:
                    terms = [gains[j] * half for half in halves]
                    if spectrum in sums:
                        terms = [s + t for s, t in zip(sums[spectrum], terms)]
                    sums[spectrum] = terms
            if position >= 0:
                total = jnp.concatenate(sums.pop(position), axis=0)
                high = total.astype(jnp.bfloat16)
                low = (total - high.astype(jnp.float32)).astype(jnp.bfloat16)
                target = pl.ds(position * in_rows + row, ROWS)
                parts_ref[target, pl.ds(lane, LANES)] = high
                parts_ref[target, pl.ds(length + lane, LANES)] = low
        return carry

    lax.fori_loop(0, in_rows // ROWS * tiles, filter_tile, 0)

    for spectrum in range(STEP):
        part = parts_ref[pl.ds(spectrum * in_rows, in_rows), :]
        product = jnp.dot(part, table_ref[...], preferred_element_type=jnp.float32).T
        turn_ref[pl.ds(spectrum, width, stride=STEP), :] = product[:width] + product[width:]
    out_ref[...] = turn_ref[...].reshape(width, STEP, in_rows).astype(jnp.bfloat16)


def spectra(previous, prev_index, voltages, first, count, coeff, table, length):
    taps = coeff.shape[0] // 8
    in_rows = voltages.shape[0]
    width = table.shape[1] // 2
    prev_cols, prev_map = prev_index
    body = functools.partial(spectra_kernel, taps=taps, length=length, offset=prev_cols // length)
    return pl.pallas_call(
        body,
        grid=(count // STEP,),
        in_specs=[
            pl.BlockSpec((in_rows, prev_cols), prev_map),
            pl.BlockSpec((in_rows, STEP * length), lambda k: (0, k + first // STEP)),
            pl.BlockSpec(coeff.shape, lambda k: (0, 0)),
            pl.BlockSpec(table.shape, lambda k: (0, 0)),
        ],
        out_specs=pl.BlockSpec((width, STEP, in_rows), lambda k: (0, k, 0)),
        out_shape=jax.ShapeDtypeStruct((width, count, in_rows), jnp.bfloat16),
        scratch_shapes=[
            pltpu.VMEM((STEP * in_rows, 2 * length), jnp.bfloat16),
            pltpu.VMEM((width * STEP, in_rows), jnp.float32),
        ],
        compiler_params=pltpu.CompilerParams(vmem_limit_bytes=VMEM_LIMIT),
    )(previous, voltages, coeff, table)


def correlate_kernel(*refs, groups_tm):
    received, (out_ref, stack_ref) = refs[:-2], refs[-2:]
    block = out_ref.shape[2]
    depth = stack_ref.shape[0]
    half = depth // 2

    @pl.when(pl.program_id(0) == 0)
    def _():
        at = 0
        for part in range(2):
            for ref in received:
                sources, _, count, in_rows = ref.shape
                for source in range(sources):
                    group, slab = divmod(source, groups_tm)
                    start = at + slab * count
                    stack_ref[start : start + count, group * in_rows : (group + 1) * in_rows] = ref[source, part]
                at += groups_tm * count

    row = pl.multiple_of(pl.program_id(0) * block, block)
    turned = stack_ref[:, pl.ds(row, block)].T
    crossed = jnp.concatenate([turned[:, half:], -turned[:, :half]], axis=1)
    scale = 2.0 / depth
    everything = stack_ref[...]
    out_ref[0, 0] = jnp.dot(turned, everything, preferred_element_type=jnp.float32) * scale
    out_ref[0, 1] = jnp.dot(crossed, everything, preferred_element_type=jnp.float32) * scale


def correlate(received, groups_tm):
    sources, _, _, in_rows = received[0].shape
    inputs = sources // groups_tm * in_rows
    depth = 2 * groups_tm * sum(r.shape[2] for r in received)
    block = math.gcd(inputs, LANES)
    return pl.pallas_call(
        functools.partial(correlate_kernel, groups_tm=groups_tm),
        grid=(inputs // block,),
        in_specs=[pl.BlockSpec(r.shape, lambda k: (0, 0, 0, 0)) for r in received],
        out_specs=pl.BlockSpec((1, 2, block, inputs), lambda k: (0, 0, k, 0)),
        out_shape=jax.ShapeDtypeStruct((1, 2, inputs, inputs), jnp.float32),
        scratch_shapes=[pltpu.VMEM((depth, inputs), jnp.bfloat16)],
        compiler_params=pltpu.CompilerParams(vmem_limit_bytes=VMEM_LIMIT),
    )(*received)


def per_device(voltages, pfb_coeff):
    in_rows = voltages.shape[0]
    taps, length = pfb_coeff.shape
    spec_dev = voltages.shape[1] // length
    groups_tm = lax.axis_size("tm")
    devices = lax.axis_size("inp") * groups_tm
    channels = CH_DEV * devices
    tail = (taps - 1) * length
    history = shifted(voltages[:, voltages.shape[1] - tail :], "tm", 1)
    coeff = jnp.repeat(pfb_coeff, 8, axis=0)
    table = dft_table(channels, length)

    later = spectra(
        voltages, (STEP * length, lambda k: (0, k)), voltages, STEP, spec_dev - STEP, coeff, table, length
    )
    early = spectra(history, (tail, lambda k: (0, 0)), voltages, 0, STEP, coeff, table, length)
    sent = jnp.concatenate([early, later], axis=1)
    sent = sent.reshape(devices, 2, spec_dev, in_rows)
    received = lax.all_to_all(sent, ("inp", "tm"), split_axis=0, concat_axis=0, tiled=True)
    return correlate([received], groups_tm)


def solution(mesh):
    return jax.shard_map(
        per_device,
        mesh=mesh,
        in_specs=(P("inp", "tm"), P()),
        out_specs=P(("inp", "tm"), None, None, None),
        check_vma=False,
    )
```

time: 310 us -> 141 us (0.45)
  other arithmetic: 109 us -> 1.21 us
  Pallas kernels: 0 us -> 78.1 us
  local copies, waits for them, and re-layouts: 67.2 us -> 3.7 us
  matrix products: 43.5 us -> 0 us
  blocking collectives: 83.7 us -> 54.4 us
    add x1 -> x0, other arithmetic: 91.2 us -> none  [per_device(): filtered + pfb_coeff[tap_index][None, None, :] * extended[:, tap_index:ta...]
    pallas_call x0 -> x3, Pallas kernels: none -> 78.1 us  [the longest x2 68.2 us: spectra(): pl.pallas_call(body, grid=(count // STEP,), in_specs=[pl.BlockSpec((in_ro...]
    dot_general x2 -> x0, matrix products: 43.5 us -> none  [the longest x1 35.3 us: per_device(): jnp.einsum('cn,asn->cas', dft_table, filtered, precision=lax.Precision.HI...]
    add x1 -> x0, local copies, waits for them, and re-layouts: 34.6 us -> none  [per_device(): filtered + pfb_coeff[tap_index][None, None, :] * extended[:, tap_index:ta...]
    all_to_all x2 -> x1, blocking collectives: 83.7 us -> 54.4 us  [per_device(): lax.all_to_all(sent, ('inp', 'tm'), split_axis=0, concat_axis=0, tiled=True)]
    unnamed x3 -> x4, local copies, waits for them, and re-layouts: 22.4 us -> 0.01 us
    another operation x2 -> x0, other arithmetic: 10.3 us -> none  [the longest x1 10.3 us: correlate(): return jnp.stack([real_sum, imag_diff], axis=1) * (1.0 / spectra_all)]
    mul x2 -> x0, other arithmetic: 7.3 us -> none  [the longest x1 7.02 us: correlate(): return jnp.stack([real_sum, imag_diff], axis=1) * (1.0 / spectra_all)]
  transfers between devices with their start and end apart: 1 -> 1, of which waited for: 1 -> 0; matrix products, arithmetic and copies ran while one was open for 0% -> 1% of each run, Pallas kernels for 0% -> 41%
where the time goes in v1:
time: 141 us
  Pallas kernels  78.1 us (55%)
  blocking collectives  54.4 us (39%)
  local copies, waits for them, and re-layouts  3.7 us (3%)
  starting transfers between devices  3.69 us (3%)
    pallas_call x2, Pallas kernels, spectra(): pl.pallas_call(body, grid=(count // STEP,), in_specs=[pl.BlockSpec((in_ro...  68.2 us
    all_to_all x1, blocking collectives, per_device(): lax.all_to_all(sent, ('inp', 'tm'), split_axis=0, concat_axis=0, tiled=True)  54.4 us
    pallas_call x1, Pallas kernels, correlate(): pl.pallas_call(functools.partial(correlate_kernel, groups_tm=groups_tm),...  9.93 us
    ppermute x1, starting transfers between devices, shifted(): return lax.ppermute(block, axis, route)  3.69 us
    slice x1, local copies, waits for them, and re-layouts, per_device(): history = shifted(voltages[:, voltages.shape[1] - tail:], 'tm', 1)  2.95 us
  transfers between devices with their start and end apart: 1, of which 0 were waited for; matrix products, arithmetic and copies ran while one was open for 1% of the time, Pallas kernels for 41%

profile of v1, /device:TPU:0, one launch (start us, length us, event | category | flops | bytes accessed | tf_op | source)
XLA Modules:
  0.0 141.2 jit_solution(5831085392441506017)
XLA Ops:
  0.0 0.0 copy-start
  0.0 2.9 %slice.3 = bf16[128,7680]{1,0:T(8,128)(2,1)} slice(bf16[128,65536]{1,0:T(8,128)(2,1)} %main_ref.3), slice={[0:128], [57856:65536]} | slice | bytes 3932160 | tf_op jit(solution)/shard_map/slice | solution.py:154
  3.0 3.7 %collective-permute-start = (bf16[128,7680]{1,0:T(8,128)(2,1)}, bf16[128,7680]{1,0:T(8,128)(2,1)}, u32[]{:S(2)}, u32[]{:S(2)}) collective-permute-start(bf16[128,7680]{1,0:T(8,128)(2,1)} %slice.3), channel_id=1, source_target_pairs={{0,1},{1,2},{2,3},{4,5},{5,6},{6,7},{8,9},{9,10},{10,11},{12,13},{... | collective-permute-start | bytes 5898248 | tf_op jit(solution)/shard_map/ppermute | solution.py:22
  6.6 0.0 copy-done
  6.7 0.7 broadcast_bitcast_fusion.coeff_ref
  7.4 57.5 %shard_map.38 = bf16[64,112,128]{2,1,0:T(8,128)(2,1)} custom-call(bf16[128,65536]{1,0:T(8,128)(2,1)} %main_ref.3, bf16[128,65536]{1,0:T(8,128)(2,1)} %main_ref.3, f32[128,512]{1,0:T(8,128)} %broadcast_bitcast_fusion.coeff_ref, bf16[1024,128]{1,0:T(8,128)(2,1)} %constant.2.clone.table_ref), custom_call_target="tpu_custom_call" | custom-call | tf_op jit(solution)/shard_map/pallas_call | solution.py:84
  64.9 0.0 copy-start.1
  64.9 0.0 collective-permute-done.prev_ref
  64.9 10.7 %shard_map.37 = bf16[64,16,128]{2,1,0:T(8,128)(2,1)} custom-call(bf16[128,7680]{1,0:T(8,128)(2,1)} %collective-permute-done.prev_ref, bf16[128,65536]{1,0:T(8,128)(2,1)} %main_ref.3, f32[128,512]{1,0:T(8,128)} %broadcast_bitcast_fusion.coeff_ref, bf16[1024,128]{1,0:T(8,128)(2,1)} %constant.2.clone.table_ref), custom_call_target="tpu_custom_call" | custom-call | tf_op jit(solution)/shard_map/pallas_call | solution.py:84
  75.6 0.0 copy-done.1
  75.6 1.2 pad_maximum_fusion
  76.8 54.4 %all_to_all.5.refs_0_ = bf16[32,2,128,128]{3,2,1,0:T(8,128)(2,1)} all-to-all(bf16[32,2,128,128]{3,2,1,0:T(8,128)(2,1)S(1)} %bitcast.3), channel_id=1, replica_groups=mesh['inp'=8,'tm'=4] {'inp','tm'}, dimensions={0} | all-to-all | bytes 4194304 | tf_op jit(solution)/shard_map/all_to_all | solution.py:164
  131.2 9.9 %shard_map.39 = f32[1,2,1024,1024]{3,2,1,0:T(8,128)} custom-call(bf16[32,2,128,128]{3,2,1,0:T(8,128)(2,1)} %all_to_all.5.refs_0_), custom_call_target="tpu_custom_call" | custom-call | tf_op jit(solution)/shard_map/pallas_call | solution.py:135
Async XLA Ops:
  0.0 6.6 %copy-start = (f32[16,512]{1,0:T(8,128)S(1)}, f32[16,512]{1,0:T(8,128)}, u32[]{:S(2)}) copy-start(f32[16,512]{1,0:T(8,128)} %param.4) | copy-start | bytes 98308
  3.0 61.9 %collective-permute-start = (bf16[128,7680]{1,0:T(8,128)(2,1)}, bf16[128,7680]{1,0:T(8,128)(2,1)}, u32[]{:S(2)}, u32[]{:S(2)}) collective-permute-start(bf16[128,7680]{1,0:T(8,128)(2,1)} %slice.3), channel_id=1, source_target_pairs={{0,1},{1,2},{2,3},{4,5},{5,6},{6,7},{8,9},{9,10},{10,11},{12,13},{... | collective-permute-start | bytes 5898248 | tf_op jit(solution)/shard_map/ppermute | solution.py:22
  64.9 10.7 %copy-start.1 = (bf16[64,112,128]{2,1,0:T(8,128)(2,1)S(1)}, bf16[64,112,128]{2,1,0:T(8,128)(2,1)}, u32[]{:S(2)}) copy-start(bf16[64,112,128]{2,1,0:T(8,128)(2,1)} %shard_map.38) | copy-start | bytes 5505028

commit v2 on v1

v2 whole, which is shorter than its diff:
```python
import functools
import math

import jax
import jax.numpy as jnp
import numpy as np
from jax import lax
from jax.experimental import pallas as pl
from jax.experimental.pallas import tpu as pltpu
from jax.sharding import PartitionSpec as P

CH_DEV = 1
STEP = 16
ROWS = 16
DIRECT = 2
LANES = 128
CUTS = (0, 5, 8)
VMEM_LIMIT = 60 * 1024 * 1024


def shifted(block, axis, distance):
    devices = range(lax.axis_size(axis))
    route = [(i - distance, i) for i in devices if i - distance in devices]
    return lax.ppermute(block, axis, route)


def dft_table(channels, length):
    samples = np.arange(length)
    angle = (np.arange(channels)[:, None] * samples[None, :] % length) * (2.0 * math.pi / length)
    table = np.stack([np.cos(angle), -np.sin(angle)], axis=1).reshape(2 * channels, length)
    return (table / math.sqrt(length)).T


def split_table(table):
    high = table.astype(jnp.bfloat16)
    low = (table - high.astype(np.float64)).astype(jnp.bfloat16)
    both = np.concatenate([high, low], axis=1)
    return jnp.asarray(np.concatenate([both, both], axis=0))


def tapped_table(table, coeff):
    product = coeff[:DIRECT, :, None] * jnp.asarray(table, jnp.float32)[None]
    high = lax.reduce_precision(product, exponent_bits=8, mantissa_bits=7)
    both = jnp.concatenate([high, product - high], axis=2).astype(jnp.bfloat16)
    pairs = both.reshape(DIRECT // 2, 2, *both.shape[1:])
    return jnp.concatenate([pairs[:, 0], pairs[:, 1]], axis=2)


def spectra_kernel(prev_ref, main_ref, coeff_ref, table_ref, tapped_ref, *refs, taps, length):
    in_rows = main_ref.shape[0]
    tiles = length // LANES
    groups = in_rows // ROWS
    offset = STEP
    if len(refs) > 5:
        history_ref, *refs, window_ref = refs
        offset = taps - 1

        @pl.when(pl.program_id(0) == 0)
        def _():
            window_ref[...] = history_ref[...]

        @pl.when(pl.program_id(0) > 0)
        def _():
            window_ref[...] = prev_ref[:, (STEP - offset) * length :]

        prev_ref = window_ref
    out_ref, even_ref, odd_ref, product_ref, turn_ref = refs
    width = out_ref.shape[0]

    def block_at(position, row, lane):
        ref, first = (main_ref, position) if position >= 0 else (prev_ref, position + offset)
        return ref[pl.ds(row, ROWS), first * length + lane : first * length + lane + LANES].astype(jnp.float32)

    def samples_at(position, row):
        ref, first = (main_ref, position) if position >= 0 else (prev_ref, position + offset)
        return ref[pl.ds(row, ROWS), first * length : (first + 1) * length]

    def filter_rows(group, parts_ref, lane):
        row = pl.multiple_of(group * ROWS, ROWS)
        gains = [coeff_ref[8 * j : 8 * j + 8, lane : lane + LANES] for j in range(taps)]
        sums = {}
        for position in range(1 - taps + DIRECT, STEP):
            block = block_at(position, row, lane)
            halves = [block[8 * k : 8 * k + 8] for k in range(ROWS // 8)]
            for j in range(DIRECT, taps):
                spectrum = position + taps - 1 - j
                if 0 <= spectrum < STEP:
                    terms = [gains[j] * half for half in halves]
                    if spectrum in sums:
                        terms = [s + t for s, t in zip(sums[spectrum], terms)]
                    sums[spectrum] = terms
            if position >= 0:
                total = jnp.concatenate(sums.pop(position), axis=0)
                high = total.astype(jnp.bfloat16)
                low = (total - high.astype(jnp.float32)).astype(jnp.bfloat16)
                target = slice(position * ROWS, position * ROWS + ROWS)
                parts_ref[target, lane : lane + LANES] = high
                parts_ref[target, length + lane : length + lane + LANES] = low

    def transform(group, parts_ref, part, parts):
        row = pl.multiple_of(group * ROWS, ROWS)
        count = STEP // parts
        start = part * count
        total = jnp.dot(
            parts_ref[start * ROWS : (start + count) * ROWS, :], table_ref[...], preferred_element_type=jnp.float32
        )
        columns = total.shape[1]
        for pair in range(DIRECT // 2):
            first = start + 1 - taps + 2 * pair
            samples = jnp.concatenate([samples_at(first + k, row) for k in range(count + 1)], axis=0)
            both = jnp.dot(samples, tapped_ref[pair], preferred_element_type=jnp.float32)
            total = total + both[: count * ROWS, :columns] + both[ROWS:, columns:]
        for k in range(count):
            product_ref[start + k, pl.ds(row, ROWS), :] = total[k * ROWS : k * ROWS + ROWS]

    def two_groups(pair, carry):
        before = jnp.where(pair == 0, groups - 1, 2 * pair - 1)
        for tile in range(tiles):
            filter_rows(2 * pair, even_ref, tile * LANES)
            if tile == 0:
                transform(before, odd_ref, 0, 1)
        for tile in range(tiles):
            filter_rows(2 * pair + 1, odd_ref, tile * LANES)
            if tile == 0:
                transform(2 * pair, even_ref, 0, 1)
        return carry

    lax.fori_loop(0, groups // 2, two_groups, 0)
    transform(groups - 1, odd_ref, 0, 1)

    for spectrum in range(STEP):
        product = product_ref[spectrum].T
        turn_ref[pl.ds(spectrum, width, stride=STEP), :] = product[:width] + product[width:]
    out_ref[...] = turn_ref[...].reshape(width, STEP, in_rows).astype(jnp.bfloat16)


def spectra(voltages, first, last, coeff, table, tapped, length, history):
    taps = coeff.shape[0] // 8
    in_rows = voltages.shape[0]
    width = table.shape[1] // 2
    wide = (in_rows, STEP * length)
    operands = [voltages, voltages, coeff, table, tapped]
    in_specs = [
        pl.BlockSpec(wide, lambda k: (0, jnp.maximum(k + first - 1, 0))),
        pl.BlockSpec(wide, lambda k: (0, k + first)),
        pl.BlockSpec(coeff.shape, lambda k: (0, 0)),
        pl.BlockSpec(table.shape, lambda k: (0, 0)),
        pl.BlockSpec(tapped.shape, lambda k: (0, 0, 0)),
    ]
    scratch = [
        pltpu.VMEM((STEP * ROWS, 2 * length), jnp.bfloat16),
        pltpu.VMEM((STEP * ROWS, 2 * length), jnp.bfloat16),
        pltpu.VMEM((STEP, in_rows, 2 * width), jnp.float32),
        pltpu.VMEM((width * STEP, in_rows), jnp.float32),
    ]
    if first == 0:
        operands.append(history)
        in_specs.append(pl.BlockSpec(history.shape, lambda k: (0, 0)))
        scratch.append(pltpu.VMEM(history.shape, history.dtype))
    return pl.pallas_call(
        functools.partial(spectra_kernel, taps=taps, length=length),
        grid=(last - first,),
        in_specs=in_specs,
        out_specs=pl.BlockSpec((width, STEP, in_rows), lambda k: (0, k, 0)),
        out_shape=jax.ShapeDtypeStruct((width, (last - first) * STEP, in_rows), jnp.bfloat16),
        scratch_shapes=scratch,
        compiler_params=pltpu.CompilerParams(vmem_limit_bytes=VMEM_LIMIT),
    )(*operands)


def correlate_kernel(*refs, groups_tm, scale, with_base):
    received, (out_ref, stack_ref) = refs[with_base:-2], refs[-2:]
    block = out_ref.shape[2]
    half = stack_ref.shape[0] // 2

    @pl.when(pl.program_id(0) == 0)
    def _():
        at = 0
        for part in range(2):
            for ref in received:
                sources, _, count, in_rows = ref.shape
                for source in range(sources):
                    group, slab = divmod(source, groups_tm)
                    start = at + slab * count
                    stack_ref[start : start + count, group * in_rows : (group + 1) * in_rows] = ref[source, part]
                at += groups_tm * count

    row = pl.multiple_of(pl.program_id(0) * block, block)
    turned = stack_ref[:, pl.ds(row, block)].T
    crossed = jnp.concatenate([turned[:, half:], -turned[:, :half]], axis=1)
    everything = stack_ref[...]
    for index, left in enumerate((turned, crossed)):
        total = jnp.dot(left, everything, preferred_element_type=jnp.float32) * scale
        out_ref[0, index] = total + refs[0][0, index] if with_base else total


def correlate(received, groups_tm, spectra_all, base=None):
    sources, _, _, in_rows = received[0].shape
    inputs = sources // groups_tm * in_rows
    depth = 2 * groups_tm * sum(r.shape[2] for r in received)
    block = math.gcd(inputs, LANES)
    rows = pl.BlockSpec((1, 2, block, inputs), lambda k: (0, 0, k, 0))
    bases = [] if base is None else [base]
    body = functools.partial(correlate_kernel, groups_tm=groups_tm, scale=1.0 / spectra_all, with_base=len(bases))
    return pl.pallas_call(
        body,
        grid=(inputs // block,),
        in_specs=[rows for _ in bases] + [pl.BlockSpec(r.shape, lambda k: (0, 0, 0, 0)) for r in received],
        out_specs=rows,
        out_shape=jax.ShapeDtypeStruct((1, 2, inputs, inputs), jnp.float32),
        scratch_shapes=[pltpu.VMEM((depth, inputs), jnp.bfloat16)],
        compiler_params=pltpu.CompilerParams(vmem_limit_bytes=VMEM_LIMIT),
    )(*bases, *received)


def per_device(voltages, pfb_coeff):
    in_rows = voltages.shape[0]
    taps, length = pfb_coeff.shape
    spec_dev = voltages.shape[1] // length
    groups_tm = lax.axis_size("tm")
    devices = lax.axis_size("inp") * groups_tm
    channels = CH_DEV * devices
    tail = (taps - 1) * length
    history = shifted(voltages[:, voltages.shape[1] - tail :], "tm", 1)
    coeff = jnp.repeat(pfb_coeff, 8, axis=0)
    exact = dft_table(channels, length)
    table = split_table(exact)
    tapped = tapped_table(exact, pfb_coeff)

    steps = spec_dev // STEP
    cuts = [steps - steps * share // 8 for share in CUTS]
    received = []
    for first, last in zip(cuts[1:], cuts[:-1]):
        sent = spectra(voltages, first, last, coeff, table, tapped, length, history)
        if last == steps:
            sent, history = lax.optimization_barrier((sent, history))
        sent = sent.reshape(devices, 2, sent.shape[1], in_rows)
        received.append(lax.all_to_all(sent, ("inp", "tm"), split_axis=0, concat_axis=0, tiled=True))
    spectra_all = spec_dev * groups_tm
    partial = correlate(received[:-1], groups_tm, spectra_all)
    return correlate(received[-1:], groups_tm, spectra_all, partial)


def solution(mesh):
    return jax.shard_map(
        per_device,
        mesh=mesh,
        in_specs=(P("inp", "tm"), P()),
        out_specs=P(("inp", "tm"), None, None, None),
        check_vma=False,
    )
```

time: 141 us -> 122 us (0.87)
  blocking collectives: 54.4 us -> 0 us
  waiting for transfers between devices: 0.01 us -> 18.6 us
  starting transfers between devices: 3.69 us -> 13.2 us
  Pallas kernels: 78.1 us -> 83.5 us
    all_to_all x1 -> x0, blocking collectives: 54.4 us -> none  [per_device(): lax.all_to_all(sent, ('inp', 'tm'), split_axis=0, concat_axis=0, tiled=True)]
    all_to_all x0 -> x2, waiting for transfers between devices: none -> 18.6 us  [per_device(): lax.all_to_all(sent, ('inp', 'tm'), split_axis=0, concat_axis=0, tiled=True)]
    all_to_all x0 -> x2, starting transfers between devices: none -> 10.6 us  [per_device(): lax.all_to_all(sent, ('inp', 'tm'), split_axis=0, concat_axis=0, tiled=True)]
    pallas_call x3 -> x4, Pallas kernels: 78.1 us -> 83.5 us  [the longest x2 63.7 us: spectra(): pl.pallas_call(functools.partial(spectra_kernel, taps=taps, length=length...]
  transfers between devices with their start and end apart: 1 -> 3, of which waited for: 0 -> 2; matrix products, arithmetic and copies ran while one was open for 1% -> 1% of each run, Pallas kernels for 41% -> 60%
where the time goes in v2:
time: 122 us; the launch traced here: 121 us
  Pallas kernels  83.5 us (68%)
  waiting for transfers between devices  18.6 us (15%)
  starting transfers between devices  13.2 us (11%)
  local copies, waits for them, and re-layouts  4.69 us (4%)
    pallas_call x2, Pallas kernels, spectra(): pl.pallas_call(functools.partial(spectra_kernel, taps=taps, length=length...  63.7 us
    pallas_call x2, Pallas kernels, correlate(): pl.pallas_call(body, grid=(inputs // block,), in_specs=[rows for _ in bas...  19.9 us
    all_to_all x2, waiting for transfers between devices, per_device(): lax.all_to_all(sent, ('inp', 'tm'), split_axis=0, concat_axis=0, tiled=True)  18.6 us
    all_to_all x2, starting transfers between devices, per_device(): lax.all_to_all(sent, ('inp', 'tm'), split_axis=0, concat_axis=0, tiled=True)  10.6 us
    slice x1, local copies, waits for them, and re-layouts, per_device(): history = shifted(voltages[:, voltages.shape[1] - tail:], 'tm', 1)  2.99 us
    ppermute x1, starting transfers between devices, shifted(): return lax.ppermute(block, axis, route)  2.64 us
  transfers between devices with their start and end apart: 3, of which 2 were waited for; matrix products, arithmetic and copies ran while one was open for 1% of the time, Pallas kernels for 60%

profile of v2, /device:TPU:0, one launch (start us, length us, event | category | flops | bytes accessed | tf_op | source)
XLA Modules:
  0.0 121.3 jit_solution(9271974127684659683)
XLA Ops:
  0.0 0.0 copy-start.3
  0.0 0.0 slice-start
  0.0 3.0 %slice.15 = bf16[128,7680]{1,0:T(8,128)(2,1)} slice(bf16[128,65536]{1,0:T(8,128)(2,1)} %main_ref.3), slice={[0:128], [57856:65536]} | slice | bytes 3932160 | tf_op jit(solution)/shard_map/slice | solution.py:224
  3.0 0.0 copy-start.4
  3.0 2.6 %collective-permute-start = (bf16[128,7680]{1,0:T(8,128)(2,1)}, bf16[128,7680]{1,0:T(8,128)(2,1)S(1)}, u32[]{:S(2)}, u32[]{:S(2)}) collective-permute-start(bf16[128,7680]{1,0:T(8,128)(2,1)} %slice.15), channel_id=1, source_target_pairs={{0,1},{1,2},{2,3},{4,5},{5,6},{6,7},{8,9},{9,10},{10,11},{12,13},{... | collective-permute-start | bytes 5898248 | tf_op jit(solution)/shard_map/ppermute | solution.py:24
  5.6 0.0 copy-done.3
  5.7 0.0 slice-done
  5.7 0.2 fusion.2
  5.9 0.1 fusion.4
  6.0 0.7 pad_maximum_fusion.tapped_ref
  6.8 0.0 copy-done.4
  6.8 0.7 broadcast_bitcast_fusion.coeff_ref
  7.5 38.6 %shard_map.46 = bf16[64,80,128]{2,1,0:T(8,128)(2,1)} custom-call(bf16[128,65536]{1,0:T(8,128)(2,1)} %main_ref.3, bf16[128,65536]{1,0:T(8,128)(2,1)} %main_ref.3, f32[128,512]{1,0:T(8,128)} %broadcast_bitcast_fusion.coeff_ref, bf16[1024,128]{1,0:T(8,128)(2,1)} %constant.4.clone.table_ref, bf16[1,512,256]{2,1,0:T(8,128)(2,1)} %pad_maximum_fusion.tapped_ref), custom_call_target="tpu_custom_call" | custom-call | tf_op jit(solution)/shard_map/pallas_call | solution.py:160
  46.1 0.0 collective-permute-done.refs_0_
  46.1 7.0 %all-to-all-start = ((bf16[32,2,80,128]{3,2,1,0:T(8,128)(2,1)}), bf16[32,2,80,128]{3,2,1,0:T(8,128)(2,1)S(1)}, u32[]{:S(2)}, u32[]{:S(2)}) async-start(bf16[32,2,80,128]{3,2,1,0:T(8,128)(2,1)} %bitcast.12), calls=%async_computation | async-start | bytes 2621440 | tf_op jit(solution)/shard_map/all_to_all | solution.py:238
  53.1 0.0 copy-done.2
  53.1 25.1 %shard_map.48 = bf16[64,48,128]{2,1,0:T(8,128)(2,1)} custom-call(bf16[128,65536]{1,0:T(8,128)(2,1)} %main_ref.3, bf16[128,65536]{1,0:T(8,128)(2,1)} %main_ref.3, f32[128,512]{1,0:T(8,128)} %broadcast_bitcast_fusion.coeff_ref, bf16[1024,128]{1,0:T(8,128)(2,1)} %constant.4.clone.table_ref, bf16[1,512,256]{2,1,0:T(8,128)(2,1)} %pad_maximum_fusion.tapped_ref, ...), custom_call_target="tpu_custom_call" | custom-call | tf_op jit(solution)/shard_map/pallas_call | solution.py:160
  78.2 6.8 %all-to-all-done.refs_0_ = bf16[32,2,80,128]{3,2,1,0:T(8,128)(2,1)S(1)} async-done(((bf16[32,2,80,128]{3,2,1,0:T(8,128)(2,1)}), bf16[32,2,80,128]{3,2,1,0:T(8,128)(2,1)S(1)}, u32[]{:S(2)}, u32[]{:S(2)}) %all-to-all-start) | async-done | bytes 1310752 | tf_op jit(solution)/shard_map/all_to_all | solution.py:238
  85.0 3.6 %all-to-all-start.1 = ((bf16[32,2,48,128]{3,2,1,0:T(8,128)(2,1)}), bf16[32,2,48,128]{3,2,1,0:T(8,128)(2,1)S(1)}, u32[]{:S(2)}, u32[]{:S(2)}) async-start(bf16[32,2,48,128]{3,2,1,0:T(8,128)(2,1)} %bitcast.13), calls=%async_computation.1 | async-start | bytes 1572864 | tf_op jit(solution)/shard_map/all_to_all | solution.py:238
  88.6 0.0 copy-done
  88.7 8.8 %shard_map.47.refs_0_ = f32[1,2,1024,1024]{3,2,1,0:T(8,128)} custom-call(bf16[32,2,80,128]{3,2,1,0:T(8,128)(2,1)} %copy-done), custom_call_target="tpu_custom_call" | custom-call | tf_op jit(solution)/shard_map/pallas_call | solution.py:205
  97.4 11.8 %all-to-all-done.1.refs_1_ = bf16[32,2,48,128]{3,2,1,0:T(8,128)(2,1)S(1)} async-done(((bf16[32,2,48,128]{3,2,1,0:T(8,128)(2,1)}), bf16[32,2,48,128]{3,2,1,0:T(8,128)(2,1)S(1)}, u32[]{:S(2)}, u32[]{:S(2)}) %all-to-all-start.1) | async-done | bytes 786464 | tf_op jit(solution)/shard_map/all_to_all | solution.py:238
  109.2 1.0 copy-done.1
  110.2 11.1 %shard_map.49 = f32[1,2,1024,1024]{3,2,1,0:T(8,128)} custom-call(f32[1,2,1024,1024]{3,2,1,0:T(8,128)} %shard_map.47.refs_0_, bf16[32,2,48,128]{3,2,1,0:T(8,128)(2,1)} %copy-done.1), custom_call_target="tpu_custom_call" | custom-call | tf_op jit(solution)/shard_map/pallas_call | solution.py:205
  (3 shorter events, 0.0 us)
Async XLA Ops:
  0.0 5.6 %copy-start.3 = (f32[512,64]{1,0:T(8,128)S(1)}, f32[512,64]{1,0:T(8,128)}, u32[]{:S(2)}) copy-start(f32[512,64]{1,0:T(8,128)} %constant.5.clone) | copy-start | bytes 393220
  0.0 5.7 %slice-start = ((f32[16,512]{1,0:T(8,128)}), f32[2,512]{1,0:T(2,128)S(1)}, s32[]{:S(2)}) async-start(f32[16,512]{1,0:T(8,128)} %param.5), calls=%async_computation.2 | async-start | bytes 8192 | tf_op jit(solution)/shard_map/slice | solution.py:42
  3.0 3.8 %copy-start.4 = (f32[16,512]{1,0:T(8,128)S(1)}, f32[16,512]{1,0:T(8,128)}, u32[]{:S(2)}) copy-start(f32[16,512]{1,0:T(8,128)} %param.5) | copy-start | bytes 98308
  3.0 43.1 %collective-permute-start = (bf16[128,7680]{1,0:T(8,128)(2,1)}, bf16[128,7680]{1,0:T(8,128)(2,1)S(1)}, u32[]{:S(2)}, u32[]{:S(2)}) collective-permute-start(bf16[128,7680]{1,0:T(8,128)(2,1)} %slice.15), channel_id=1, source_target_pairs={{0,1},{1,2},{2,3},{4,5},{5,6},{6,7},{8,9},{9,10},{10,11},{12,13},{... | collective-permute-start | bytes 5898248 | tf_op jit(solution)/shard_map/ppermute | solution.py:24
  46.1 7.0 %copy-start.2 = (bf16[128,7680]{1,0:T(8,128)(2,1)}, bf16[128,7680]{1,0:T(8,128)(2,1)S(1)}, u32[]{:S(2)}) copy-start(bf16[128,7680]{1,0:T(8,128)(2,1)S(1)} %collective-permute-done.refs_0_) | copy-start | bytes 5898244
  46.1 38.9 %all-to-all-start = ((bf16[32,2,80,128]{3,2,1,0:T(8,128)(2,1)}), bf16[32,2,80,128]{3,2,1,0:T(8,128)(2,1)S(1)}, u32[]{:S(2)}, u32[]{:S(2)}) async-start(bf16[32,2,80,128]{3,2,1,0:T(8,128)(2,1)} %bitcast.12), calls=%async_computation | async-start | bytes 2621440 | tf_op jit(solution)/shard_map/all_to_all | solution.py:238
  85.0 3.6 %copy-start = (bf16[32,2,80,128]{3,2,1,0:T(8,128)(2,1)}, bf16[32,2,80,128]{3,2,1,0:T(8,128)(2,1)S(1)}, u32[]{:S(2)}) copy-start(bf16[32,2,80,128]{3,2,1,0:T(8,128)(2,1)S(1)} %all-to-all-done.refs_0_) | copy-start | bytes 3932164
  85.0 24.2 %all-to-all-start.1 = ((bf16[32,2,48,128]{3,2,1,0:T(8,128)(2,1)}), bf16[32,2,48,128]{3,2,1,0:T(8,128)(2,1)S(1)}, u32[]{:S(2)}, u32[]{:S(2)}) async-start(bf16[32,2,48,128]{3,2,1,0:T(8,128)(2,1)} %bitcast.13), calls=%async_computation.1 | async-start | bytes 1572864 | tf_op jit(solution)/shard_map/all_to_all | solution.py:238
  109.2 1.0 copy-start.1
